TPU v7x, 256 devices: a whole 4x4x8 slice. The times are simulated.
256 devices in a mesh: row: 16 (over y, z_hi), col: 16 (over x, z_lo, core).
Axes of the slice: x: 4, y: 4, z: 8 (z_hi: 4, z_lo: 2; z = z_hi * 2 + z_lo), core: 2. Of those that a mesh axis runs over, the one named last changes fastest.
Arguments:
- left_act: bfloat16 [1536, 128], P(('row', 'col')), may hold values from -540 to 540
- right_act: bfloat16 [1536, 128], P(('row', 'col')), may hold values from -6 to 6
- norm_gain: float32 [128], replicated, may hold values from 0.25 to 1.75
- norm_bias: float32 [128], replicated, may hold values from -3 to 3
- w_in: bfloat16 [128, 512], replicated, may hold values from -0.5 to 0.5
- b_in: float32 [512], replicated, may hold values from -3 to 3
- w_out: bfloat16 [512, 128], replicated, may hold values from -0.25 to 0.25
- w_bins: bfloat16 [128, 64], replicated, may hold values from -0.5 to 0.5
- labels: int32 [1536, 1536], P('row', 'col'), may hold values from 0 to 63, as said below
Outputs:
- grad_left: float32 [1536, 128], P(('row', 'col'))
- grad_right: float32 [1536, 128], P('col')
- grad_w_in: float32 [128, 512], replicated
- grad_w_out: float32 [512, 128], replicated
- grad_w_bins: float32 [128, 64], replicated
Inputs may be any that keep to these rules, and one draw needn't show every extreme that they name: labels is symmetric: labels[i, j] equals labels[j, i].
All inputs are finite; a program needn't handle non-finite values.
Results may differ from a plain program's by a relative error of at most 0.00039.
Values may be sent and summed in bfloat16 or wider, within the bound.
No kernel may reach another device: no remote copies, remote signals or barrier semaphores. Data moves between devices by JAX's collectives and lax.ppermute only.
A program may use at most 64 MiB of HBM per device.

v0:
```python
import functools

import jax
import jax.numpy as jnp
from jax import lax
from jax.experimental import pallas as pl
from jax.experimental.pallas import tpu as pltpu
from jax.sharding import PartitionSpec as P


GROUP = 8
F32 = jnp.float32
BF16 = jnp.bfloat16


def from_everyone(value, axis):
    count = lax.axis_size(axis)
    return lax.all_to_all(
        jnp.broadcast_to(value[None], (count, *value.shape)), axis, 0, 0, tiled=True
    )


def inner(first, second):
    return lax.dot_general(first, second, (((0,), (0,)), ((), ())), preferred_element_type=F32)


def outer(first, second):
    return lax.dot_general(first, second, (((1,), (1,)), ((), ())), preferred_element_type=F32)


def dot(first, second):
    return jnp.dot(first, second, preferred_element_type=F32)


def twin_swap(size, count):
    return [(a * count + b, b * count + a) for a in range(size) for b in range(count)]


def block_routes(size, count):
    if (size, count) != (16, 16):
        return twin_swap(size, count)
    pairs = []
    for r in range(size):
        for c in range(count):
            y, z = (r // 4 - c // 4) % 4, (r % 4 - c % 4) % 4
            low = (c // 2) % 2
            low = (low, 1, 1 - low, 0)[z]
            k = 4 * ((c // 4 + 2 - y) % 4) + 2 * low + (z + 1) % 2
            pairs.append((c * count + k, r * count + c))
    return pairs


def pair_kernel(
    place,
    mine_ref,
    theirs_ref,
    labels_ref,
    gain_ref,
    bias_ref,
    w_in_ref,
    b_in_ref,
    w_out_ref,
    w_bins_ref,
    col_out,
    own_left,
    far_right,
    far_left,
    own_right,
    w_in_half,
    w_out_half,
    blk,
    blk_center,
    far_side,
    far_center,
    label_rows,
    grad_in,
    grad_out_t,
    grad_bins,
    side_sums,
    *,
    count,
    rows,
):
    block = count * rows
    half = block // 2
    width = gain_ref.shape[1]
    beyond = half + GROUP
    twin = place[0] == place[1]
    skew = (place[0] > place[1]).astype(jnp.int32)

    for m in range(count):
        one = mine_ref[m].astype(F32)
        other = theirs_ref[m].astype(F32)
        for side in range(2):
            at = side * GROUP
            blk[side, m * rows : (m + 1) * rows, :] = one[at : at + rows]
            far_side[side, m * rows : (m + 1) * rows, :] = other[at : at + rows]
    label_rows[0:block, :] = labels_ref[...]
    label_rows[block:, :] = labels_ref[0:beyond, :]
    for side in range(2):
        value = blk[side]
        blk_center[side] = value - jnp.mean(value, axis=-1, keepdims=True)
        value = far_side[side, 0:block, :]
        value = value - jnp.mean(value, axis=-1, keepdims=True)
        far_center[side, 0:block, :] = value
        far_center[side, block:, :] = value[0:beyond]
        far_side[side, block:, :] = far_side[side, 0:beyond, :]

    grad_in[...] = jnp.zeros_like(grad_in)
    grad_out_t[...] = jnp.zeros_like(grad_out_t)
    grad_bins[...] = jnp.zeros_like(grad_bins)
    side_sums[...] = jnp.zeros_like(side_sums)

    w_in_half[...] = w_in_ref[...] * jnp.asarray(0.5, BF16)
    w_out_half[...] = w_out_ref[...] * jnp.asarray(0.5, BF16)
    gain = gain_ref[...]
    bias = bias_ref[...]
    b_in = 0.5 * b_in_ref[...]
    sub = lax.broadcasted_iota(jnp.int32, (GROUP, width), 0)
    lane = lax.broadcasted_iota(jnp.int32, (GROUP, width), 1)
    near = [sub >= ii + skew for ii in range(GROUP)]
    bin_lane = lax.broadcasted_iota(jnp.int32, (GROUP, w_bins_ref.shape[1]), 1).astype(F32)
    span = GROUP * half
    every = span + GROUP

    def step(s, carry):
        first = pl.multiple_of(s * GROUP, GROUP)

        def head(ref, *lead):
            return ref[(*lead, pl.ds(first, GROUP), slice(None))]

        def middle(ref, *lead):
            return ref[(*lead, pl.ds(first + GROUP, half - GROUP), slice(None))]

        def away(ref, *lead):
            return ref[(*lead, pl.ds(first + half, GROUP), slice(None))]

        summed, center = [], []
        for mine, other, into in ((blk, far_side, summed), (blk_center, far_center, center)):
            for side in range(2):
                own = head(mine, side)
                close, apart = head(other, 1 - side), away(other, 1 - side)
                rest = middle(other, 1 - side) if half > GROUP else None
                for ii in range(GROUP):
                    one = own[ii : ii + 1, :]
                    into.append(jnp.where(near[ii], close, apart) + one)
                    if half > GROUP:
                        into.append(rest + one)
                into.append(own + apart)
        summed = jnp.concatenate(summed, axis=0)
        center = jnp.concatenate(center, axis=0)
        inv_scale = lax.rsqrt(jnp.mean(center * center, axis=-1, keepdims=True) + 1e-05)
        normal_form = center * inv_scale
        normed = (normal_form * gain + bias).astype(BF16)
        act = dot(normed, w_in_half[...]) + b_in
        up = jnp.tanh(act) + 1.0
        hidden = (act * up).astype(BF16)
        slope = up * (act * (2.0 - up) + 1.0)
        updated = (summed + dot(hidden, w_out_ref[...])).astype(BF16)
        logits = dot(updated, w_bins_ref[...])
        sym = logits[0:every] + logits[every:]

        hots, scales = [], []
        label_close, label_apart = head(label_rows), away(label_rows)
        if half > GROUP:
            label_rest = middle(label_rows)
            wide = lax.broadcasted_iota(jnp.int32, label_rest.shape, 1)
            plain = jnp.full((half - GROUP, 1), 2.0, F32)
        for ii in range(GROUP):
            chosen = jnp.where(near[ii], label_close, label_apart)
            hots.append(
                jnp.sum(jnp.where(lane == first + ii, chosen, 0.0), axis=-1, keepdims=True)
            )
            scales.append(jnp.where((sub[:, 0:1] == ii) & twin, 1.0, 2.0))
            if half > GROUP:
                hots.append(
                    jnp.sum(jnp.where(wide == first + ii, label_rest, 0.0), axis=-1, keepdims=True)
                )
                scales.append(plain)
        hots.append(
            jnp.sum(jnp.where(lane == first + sub, label_apart, 0.0), axis=-1, keepdims=True)
        )
        scales.append(jnp.where((sub[:, 0:1] >= 0) & twin, 1.0, 0.0))
        hot = jnp.concatenate(hots, axis=0)
        scale = jnp.concatenate(scales, axis=0)
        lanes = jnp.broadcast_to(bin_lane[0:1], sym.shape)
        expo = jnp.exp(sym - jnp.max(sym, axis=-1, keepdims=True))
        probs = expo / jnp.sum(expo, axis=-1, keepdims=True)
        logit_grad = (scale * (probs - jnp.where(lanes == hot, 1.0, 0.0))).astype(BF16)

        upd_grad = outer(logit_grad, w_bins_ref[...])
        upd_half = upd_grad.astype(BF16)
        grad_bins[...] += inner(updated[0:every], logit_grad) + inner(updated[every:], logit_grad)
        grad_out_t[...] += inner(upd_half, hidden[0:every]) + inner(upd_half, hidden[every:])
        hid_grad = outer(upd_half, w_out_half[...])
        pre_grad = jnp.concatenate(
            [(hid_grad * slope[0:every]).astype(BF16), (hid_grad * slope[every:]).astype(BF16)],
            axis=0,
        )
        grad_in[...] += inner(normed, pre_grad)
        norm_grad = outer(pre_grad, w_in_ref[...]) * gain
        pair_grad = inv_scale * (
            norm_grad
            - jnp.mean(norm_grad, axis=-1, keepdims=True)
            - normal_form * jnp.mean(norm_grad * normal_form, axis=-1, keepdims=True)
        )
        for side in range(2):
            mine = pair_grad[side * every : (side + 1) * every] + upd_grad
            ones, head_near, head_far, tail = [], None, None, None
            for ii in range(GROUP):
                part = mine[ii * half : (ii + 1) * half]
                ones.append(jnp.sum(part, axis=0, keepdims=True))
                close = jnp.where(near[ii], part[0:GROUP], 0.0)
                apart = part[0:GROUP] - close
                head_near = close if ii == 0 else head_near + close
                head_far = apart if ii == 0 else head_far + apart
                if half > GROUP:
                    tail = part[GROUP:] if ii == 0 else tail + part[GROUP:]
            target = (own_left, far_right)[side]
            target[pl.ds(first, GROUP), :] = jnp.concatenate(ones, axis=0) + mine[span:]
            side_sums[1 - side, pl.ds(first, GROUP), :] += head_near
            side_sums[1 - side, pl.ds(first + half, GROUP), :] += head_far + mine[span:]
            if half > GROUP:
                side_sums[1 - side, pl.ds(first + GROUP, half - GROUP), :] += tail
        return carry

    lax.fori_loop(0, block // GROUP, step, 0, unroll=2)

    for side in range(2):
        target = (far_left, own_right)[side]
        target[0:beyond, :] = side_sums[side, 0:beyond, :] + side_sums[side, block:, :]
        target[beyond:, :] = side_sums[side, beyond:block, :]

    share_in = grad_in.shape[0] // count
    share_out = grad_out_t.shape[1] // count
    tiles = grad_in.shape[1] // width
    grad_out = grad_out_t[...].T
    bins = grad_bins[...]
    bins = jnp.concatenate([bins, jnp.zeros_like(bins)], axis=1)
    for m in range(count):
        at = 0
        for t in range(tiles):
            col_out[m, at : at + share_in, :] = grad_in[
                m * share_in : (m + 1) * share_in, t * width : (t + 1) * width
            ]
            at += share_in
        col_out[m, at : at + share_out, :] = grad_out[m * share_out : (m + 1) * share_out]
        at += share_out
        col_out[m, at : at + share_in, :] = bins[m * share_in : (m + 1) * share_in]


def run_pairs(place, mine, theirs, rows, labels, gain, bias, w_in, b_in, w_out, w_bins):
    count = mine.shape[0]
    width, hidden = w_in.shape
    bins = w_bins.shape[1]
    block = count * rows
    long = block + block // 2 + GROUP
    share = (width // count) * (hidden // width) + hidden // count + width // count
    vmem = pl.BlockSpec(memory_space=pltpu.VMEM)
    smem = pl.BlockSpec(memory_space=pltpu.SMEM)
    return pl.pallas_call(
        functools.partial(pair_kernel, count=count, rows=rows),
        out_shape=(
            jax.ShapeDtypeStruct((count, share, width), F32),
            *[jax.ShapeDtypeStruct((block, width), F32)] * 4,
        ),
        in_specs=[smem] + [vmem] * 9,
        out_specs=(vmem,) * 5,
        scratch_shapes=[
            pltpu.VMEM((width, hidden), BF16),
            pltpu.VMEM((hidden, width), BF16),
            pltpu.VMEM((2, block, width), F32),
            pltpu.VMEM((2, block, width), F32),
            pltpu.VMEM((2, long, width), F32),
            pltpu.VMEM((2, long, width), F32),
            pltpu.VMEM((long, width), F32),
            pltpu.VMEM((width, hidden), F32),
            pltpu.VMEM((width, hidden), F32),
            pltpu.VMEM((width, bins), F32),
            pltpu.VMEM((2, long, width), F32),
        ],
        compiler_params=pltpu.CompilerParams(vmem_limit_bytes=56 * 1024 * 1024),
        interpret=INTERPRET,
        name="pairs",
    )(
        place,
        mine,
        theirs,
        labels,
        gain[None],
        bias[None],
        w_in,
        b_in[None],
        w_out,
        w_bins,
    )


INTERPRET = False


def on_device(left_act, right_act, norm_gain, norm_bias, w_in, b_in, w_out, w_bins, labels):
    count = lax.axis_size("col")
    size = lax.axis_size("row")
    rows, width = left_act.shape
    hidden = w_in.shape[1]
    routes = block_routes(size, count)
    back = [(there, here) for here, there in routes]
    both = ("row", "col")
    gap = jnp.zeros((GROUP - rows, width), left_act.dtype)
    stacked = jnp.concatenate([left_act, gap, right_act, gap], axis=0)
    mine = from_everyone(stacked, "col")
    theirs = lax.ppermute(mine, both, routes)
    turned = jnp.pad(labels.T.astype(F32), ((0, 0), (0, width - labels.shape[0])))
    place = jnp.stack([lax.axis_index("row"), lax.axis_index("col")]).astype(jnp.int32)
    col_out, own_left, far_right, far_left, own_right = run_pairs(
        place, mine, theirs, rows, turned, norm_gain, norm_bias, w_in, b_in, w_out, w_bins
    )
    shares = lax.all_to_all(col_out, "col", 0, 0, tiled=True)
    shares = shares.sum(axis=0)
    far_right = lax.ppermute(far_right, both, routes)
    right = own_right + far_right
    right = lax.optimization_barrier(right)
    share = shares.shape[0]
    piece = -(-share // size)
    shares = jnp.pad(shares, ((0, piece * size - share), (0, 0)))
    pieces = jnp.concatenate(
        [
            shares.reshape(size, piece, width) / (rows * count * size),
            right.reshape(size, rows, width),
        ],
        axis=1,
    )
    pieces = lax.all_to_all(pieces, "row", 0, 0, tiled=True)
    pieces = pieces.sum(axis=0)
    far_left = lax.ppermute(far_left, both, back)
    left = own_left + far_left
    left = lax.optimization_barrier(left)
    pieces = from_everyone(pieces, "row")
    grad_right = pieces[:, piece:].reshape(rows * size, width)
    last = jnp.concatenate(
        [
            jnp.broadcast_to(
                pieces[:, 0:piece].reshape(size * piece, width)[None, 0:share],
                (count, share, width),
            ),
            left.reshape(count, rows, width),
        ],
        axis=1,
    )
    last = lax.all_to_all(last, "col", 0, 0, tiled=True)
    grad_left = last[:, share:].sum(axis=0)
    cut = (width // count) * (hidden // width)
    grad_in = (
        last[:, 0:cut]
        .reshape(count, hidden // width, width // count, width)
        .transpose(0, 2, 1, 3)
        .reshape(width, hidden)
    )
    grad_out = last[:, cut : cut + hidden // count].reshape(hidden, width)
    grad_bins = last[:, cut + hidden // count : share, 0 : w_bins.shape[1]].reshape(width, -1)
    return (grad_left, grad_right, grad_in, grad_out, grad_bins)


def solution(mesh):
    placed = (
        P(("row", "col"), None),
        P(("row", "col"), None),
        P(),
        P(),
        P(),
        P(),
        P(),
        P(),
        P("row", "col"),
    )

    return jax.shard_map(
        on_device,
        mesh=mesh,
        in_specs=placed,
        out_specs=(P(("row", "col"), None), P("col", None), P(), P(), P()),
        check_vma=False,
    )
```

profile of v0, /device:TPU:1, one launch (start us, length us, event | category | flops | bytes accessed | tf_op | source)
XLA Modules:
  0.0 130.6 jit_solution(11276480732679220438)
XLA Ops:
  0.6 0.7 pad_maximum_fusion.2
  1.4 0.6 broadcast_in_dim.15
  2.0 0.0 copy-start.5
  2.0 7.3 %all-to-all-start = ((bf16[16,16,128]{2,1,0:T(8,128)(2,1)}), bf16[16,16,128]{2,1,0:T(8,128)(2,1)S(1)}, u32[]{:S(2)}, u32[]{:S(2)}) async-start(bf16[16,16,128]{2,1,0:T(8,128)(2,1)} %broadcast_in_dim.15), calls=%async_computation | async-start | bytes 131072 | tf_op jit(solution)/shard_map/all_to_all | solution.py:18
  9.3 0.0 copy-start.2
  9.3 0.0 copy-done.5
  9.3 0.7 copy.21.w_bins_ref
  10.0 0.1 copy-done.2
  10.1 0.1 copy.20
  10.2 0.6 pad.8.labels_ref
  10.8 4.3 %all-to-all-done.mine_ref = bf16[16,16,128]{2,1,0:T(8,128)(2,1)S(1)} async-done(((bf16[16,16,128]{2,1,0:T(8,128)(2,1)}), bf16[16,16,128]{2,1,0:T(8,128)(2,1)S(1)}, u32[]{:S(2)}, u32[]{:S(2)}) %all-to-all-start) | async-done | bytes 65568 | tf_op jit(solution)/shard_map/all_to_all | solution.py:18
  15.1 0.0 copy-start
  15.1 3.2 %collective-permute-start = (bf16[16,16,128]{2,1,0:T(8,128)(2,1)S(1)}, bf16[16,16,128]{2,1,0:T(8,128)(2,1)S(1)}, u32[]{:S(2)}, u32[]{:S(2)}) collective-permute-start(bf16[16,16,128]{2,1,0:T(8,128)(2,1)S(1)} %all-to-all-done.mine_ref), channel_id=1, source_target_pairs={{9,0},{24,1},{41,2},{58,3},{65,4},{80,5},{97,6},{114,7},{137,8},{1... | collective-permute-start | bytes 196616 | tf_op jit(solution)/shard_map/ppermute | solution.py:313
  18.4 0.6 pad_add_fusion.place
  18.9 3.3 %collective-permute-done.theirs_ref = bf16[16,16,128]{2,1,0:T(8,128)(2,1)S(1)} collective-permute-done((bf16[16,16,128]{2,1,0:T(8,128)(2,1)S(1)}, bf16[16,16,128]{2,1,0:T(8,128)(2,1)S(1)}, u32[]{:S(2)}, u32[]{:S(2)}) %collective-permute-start) | collective-permute-done | bytes 65568 | tf_op jit(solution)/shard_map/ppermute | solution.py:313
  22.2 0.0 copy-start.1
  22.2 0.0 copy-done
  22.2 0.6 copy-done.1
  22.8 32.3 %pairs.1 = (f32[16,72,128]{2,1,0:T(8,128)}, f32[96,128]{1,0:T(8,128)}, f32[96,128]{1,0:T(8,128)}, f32[96,128]{1,0:T(8,128)}, f32[96,128]{1,0:T(8,128)}) custom-call(s32[2]{0:T(128)} %pad_add_fusion.place, bf16[16,16,128]{2,1,0:T(8,128)(2,1)} %copy-done, bf16[16,16,128]{2,1,0:T(8,128)(2,1)} %copy-done.1, f32[96,128]{1,0:T(8,128)} %pad.8.labels_ref, ...), custom_call_target="tpu_custom_call" | custom-call | tf_op jit(solution)/shard_map/pairs/pallas_call | solution.py:261
  55.1 0.0 copy-start.7
  55.1 0.0 copy-start.4
  55.2 9.5 %all-to-all-start.1 = ((f32[16,72,128]{2,1,0:T(8,128)}), f32[16,72,128]{2,1,0:T(8,128)S(1)}, u32[]{:S(2)}, u32[]{:S(2)}) async-start(f32[16,72,128]{2,1,0:T(8,128)} %get-tuple-element.10), calls=%async_computation.1 | async-start | bytes 1179648 | tf_op jit(solution)/shard_map/all_to_all | solution.py:319
  64.7 0.0 copy-done.7
  64.7 0.1 collective-permute-start.1
  64.8 7.4 %collective-permute-done.1 = f32[96,128]{1,0:T(8,128)S(1)} collective-permute-done((f32[96,128]{1,0:T(8,128)S(1)}, f32[96,128]{1,0:T(8,128)S(1)}, u32[]{:S(2)}, u32[]{:S(2)}) %collective-permute-start.1) | collective-permute-done | bytes 49184 | tf_op jit(solution)/shard_map/ppermute | solution.py:321
  72.2 0.0 copy-done.4
  72.2 4.6 %all-to-all-done.1 = f32[16,72,128]{2,1,0:T(8,128)S(1)} async-done(((f32[16,72,128]{2,1,0:T(8,128)}), f32[16,72,128]{2,1,0:T(8,128)S(1)}, u32[]{:S(2)}, u32[]{:S(2)}) %all-to-all-start.1) | async-done | bytes 589856 | tf_op jit(solution)/shard_map/all_to_all | solution.py:319
  76.9 17.7 %all_to_all.25 = f32[16,11,128]{2,1,0:T(8,128)S(1)} all-to-all(f32[16,11,128]{2,1,0:T(8,128)S(1)} %pad_maximum_fusion.1), channel_id=1, replica_groups=mesh['row'=16,'col'=16] {'row'}, dimensions={0} | all-to-all | bytes 180224 | tf_op jit(solution)/shard_map/all_to_all | solution.py:334
  94.7 0.7 broadcast_in_dim.35
  95.3 0.0 copy-start.6
  95.3 0.0 copy-start.3
  95.3 3.6 %all-to-all-start.3 = ((f32[16,11,128]{2,1,0:T(8,128)}), f32[16,11,128]{2,1,0:T(8,128)S(1)}, u32[]{:S(2)}, u32[]{:S(2)}) async-start(f32[16,11,128]{2,1,0:T(8,128)} %broadcast_in_dim.35), calls=%async_computation.3 | async-start | bytes 262144 | tf_op jit(solution)/shard_map/all_to_all | solution.py:18
  99.0 0.0 copy-done.6
  99.0 3.9 %collective-permute-start.2 = (f32[96,128]{1,0:T(8,128)S(1)}, f32[96,128]{1,0:T(8,128)S(1)}, u32[]{:S(2)}, u32[]{:S(2)}) collective-permute-start(f32[96,128]{1,0:T(8,128)S(1)} %copy-done.6), channel_id=1, source_target_pairs={{0,9},{1,24},{2,41},{3,58},{4,65},{5,80},{6,97},{7,114},{8,137},{9... | collective-permute-start | bytes 147464 | tf_op jit(solution)/shard_map/ppermute | solution.py:336
  102.9 2.7 %collective-permute-done.2 = f32[96,128]{1,0:T(8,128)S(1)} collective-permute-done((f32[96,128]{1,0:T(8,128)S(1)}, f32[96,128]{1,0:T(8,128)S(1)}, u32[]{:S(2)}, u32[]{:S(2)}) %collective-permute-start.2) | collective-permute-done | bytes 49184 | tf_op jit(solution)/shard_map/ppermute | solution.py:336
  105.6 0.0 copy-done.3
  105.7 2.9 %all-to-all-done.3 = f32[16,11,128]{2,1,0:T(8,128)S(1)} async-done(((f32[16,11,128]{2,1,0:T(8,128)}), f32[16,11,128]{2,1,0:T(8,128)S(1)}, u32[]{:S(2)}, u32[]{:S(2)}) %all-to-all-start.3) | async-done | bytes 90144 | tf_op jit(solution)/shard_map/all_to_all | solution.py:18
  108.7 0.9 pad_maximum_fusion
  109.5 7.8 %all-to-all-start.4 = ((f32[16,78,128]{2,1,0:T(8,128)}), f32[16,78,128]{2,1,0:T(8,128)S(1)}, u32[]{:S(2)}, u32[]{:S(2)}) async-start(f32[16,78,128]{2,1,0:T(8,128)} %pad_maximum_fusion), calls=%async_computation.4 | async-start | bytes 1310720 | tf_op jit(solution)/shard_map/all_to_all | solution.py:351
  117.3 0.6 reshape.43
  118.0 10.5 %all-to-all-done.4 = f32[16,78,128]{2,1,0:T(8,128)S(1)} async-done(((f32[16,78,128]{2,1,0:T(8,128)}), f32[16,78,128]{2,1,0:T(8,128)S(1)}, u32[]{:S(2)}, u32[]{:S(2)}) %all-to-all-start.4) | async-done | bytes 639008 | tf_op jit(solution)/shard_map/all_to_all | solution.py:351
  128.4 0.7 copy.22
  129.1 0.6 slice_reduce_fusion
  129.7 0.9 fusion
  (17 shorter events, 0.2 us)
Async XLA Ops:
  2.0 7.3 %copy-start.5 = (bf16[128,64]{0,1:T(8,128)(2,1)S(1)}, bf16[128,64]{0,1:T(8,128)(2,1)}, u32[]{:S(2)}) copy-start(bf16[128,64]{0,1:T(8,128)(2,1)} %param.16) | copy-start | bytes 49156
  2.0 13.1 %all-to-all-start = ((bf16[16,16,128]{2,1,0:T(8,128)(2,1)}), bf16[16,16,128]{2,1,0:T(8,128)(2,1)S(1)}, u32[]{:S(2)}, u32[]{:S(2)}) async-start(bf16[16,16,128]{2,1,0:T(8,128)(2,1)} %broadcast_in_dim.15), calls=%async_computation | async-start | bytes 131072 | tf_op jit(solution)/shard_map/all_to_all | solution.py:18
  9.3 0.8 copy-start.2
  15.1 7.1 %copy-start = (bf16[16,16,128]{2,1,0:T(8,128)(2,1)}, bf16[16,16,128]{2,1,0:T(8,128)(2,1)S(1)}, u32[]{:S(2)}) copy-start(bf16[16,16,128]{2,1,0:T(8,128)(2,1)S(1)} %all-to-all-done.mine_ref) | copy-start | bytes 196612
  15.1 7.1 %collective-permute-start = (bf16[16,16,128]{2,1,0:T(8,128)(2,1)S(1)}, bf16[16,16,128]{2,1,0:T(8,128)(2,1)S(1)}, u32[]{:S(2)}, u32[]{:S(2)}) collective-permute-start(bf16[16,16,128]{2,1,0:T(8,128)(2,1)S(1)} %all-to-all-done.mine_ref), channel_id=1, source_target_pairs={{9,0},{24,1},{41,2},{58,3},{65,4},{80,5},{97,6},{114,7},{137,8},{1... | collective-permute-start | bytes 196616 | tf_op jit(solution)/shard_map/ppermute | solution.py:313
  22.2 0.6 copy-start.1
  55.1 9.5 %copy-start.7 = (f32[96,128]{1,0:T(8,128)S(1)}, f32[96,128]{1,0:T(8,128)}, u32[]{:S(2)}) copy-start(f32[96,128]{1,0:T(8,128)} %get-tuple-element.12) | copy-start | bytes 147460
  55.1 17.0 %copy-start.4 = (f32[96,128]{1,0:T(8,128)S(1)}, f32[96,128]{1,0:T(8,128)}, u32[]{:S(2)}) copy-start(f32[96,128]{1,0:T(8,128)} %get-tuple-element.11) | copy-start | bytes 147460
  55.2 21.7 %all-to-all-start.1 = ((f32[16,72,128]{2,1,0:T(8,128)}), f32[16,72,128]{2,1,0:T(8,128)S(1)}, u32[]{:S(2)}, u32[]{:S(2)}) async-start(f32[16,72,128]{2,1,0:T(8,128)} %get-tuple-element.10), calls=%async_computation.1 | async-start | bytes 1179648 | tf_op jit(solution)/shard_map/all_to_all | solution.py:319
  64.7 7.5 %collective-permute-start.1 = (f32[96,128]{1,0:T(8,128)S(1)}, f32[96,128]{1,0:T(8,128)S(1)}, u32[]{:S(2)}, u32[]{:S(2)}) collective-permute-start(f32[96,128]{1,0:T(8,128)S(1)} %copy-done.7), channel_id=1, source_target_pairs={{9,0},{24,1},{41,2},{58,3},{65,4},{80,5},{97,6},{114,7},{137,8},{1... | collective-permute-start | bytes 147464 | tf_op jit(solution)/shard_map/ppermute | solution.py:321
  95.3 3.7 %copy-start.6 = (f32[96,128]{1,0:T(8,128)S(1)}, f32[96,128]{1,0:T(8,128)}, u32[]{:S(2)}) copy-start(f32[96,128]{1,0:T(8,128)} %get-tuple-element.14) | copy-start | bytes 147460
  95.3 10.3 %copy-start.3 = (f32[96,128]{1,0:T(8,128)S(1)}, f32[96,128]{1,0:T(8,128)}, u32[]{:S(2)}) copy-start(f32[96,128]{1,0:T(8,128)} %get-tuple-element.13) | copy-start | bytes 147460
  95.3 13.3 %all-to-all-start.3 = ((f32[16,11,128]{2,1,0:T(8,128)}), f32[16,11,128]{2,1,0:T(8,128)S(1)}, u32[]{:S(2)}, u32[]{:S(2)}) async-start(f32[16,11,128]{2,1,0:T(8,128)} %broadcast_in_dim.35), calls=%async_computation.3 | async-start | bytes 262144 | tf_op jit(solution)/shard_map/all_to_all | solution.py:18
  99.0 6.6 %collective-permute-start.2 = (f32[96,128]{1,0:T(8,128)S(1)}, f32[96,128]{1,0:T(8,128)S(1)}, u32[]{:S(2)}, u32[]{:S(2)}) collective-permute-start(f32[96,128]{1,0:T(8,128)S(1)} %copy-done.6), channel_id=1, source_target_pairs={{0,9},{1,24},{2,41},{3,58},{4,65},{5,80},{6,97},{7,114},{8,137},{9... | collective-permute-start | bytes 147464 | tf_op jit(solution)/shard_map/ppermute | solution.py:336
  109.5 18.9 %all-to-all-start.4 = ((f32[16,78,128]{2,1,0:T(8,128)}), f32[16,78,128]{2,1,0:T(8,128)S(1)}, u32[]{:S(2)}, u32[]{:S(2)}) async-start(f32[16,78,128]{2,1,0:T(8,128)} %pad_maximum_fusion), calls=%async_computation.4 | async-start | bytes 1310720 | tf_op jit(solution)/shard_map/all_to_all | solution.py:351
where the time goes:
time: 131 us
  waiting for transfers between devices  35.7 us (27%)
  starting transfers between devices  35.5 us (27%)
  Pallas kernels  32.3 us (25%)
  blocking collectives  17.7 us (14%)
  local copies, waits for them, and re-layouts  5.72 us (4%)
  other arithmetic  2.87 us (2%)
    pallas_call x1, Pallas kernels, run_pairs(): pl.pallas_call(functools.partial(pair_kernel, count=count, rows=rows), ou...  32.3 us
    all_to_all x1, blocking collectives, on_device(): pieces = lax.all_to_all(pieces, 'row', 0, 0, tiled=True)  17.7 us
    all_to_all x2, starting transfers between devices, from_everyone(): lax.all_to_all(jnp.broadcast_to(value[None], (count, *value.shape)), axis...  10.9 us
    all_to_all x1, waiting for transfers between devices, on_device(): last = lax.all_to_all(last, 'col', 0, 0, tiled=True)  10.5 us
    all_to_all x1, starting transfers between devices, on_device(): shares = lax.all_to_all(col_out, 'col', 0, 0, tiled=True)  9.51 us
    all_to_all x1, starting transfers between devices, on_device(): last = lax.all_to_all(last, 'col', 0, 0, tiled=True)  7.77 us
    ppermute x1, waiting for transfers between devices, on_device(): far_right = lax.ppermute(far_right, both, routes)  7.36 us
    all_to_all x2, waiting for transfers between devices, from_everyone(): lax.all_to_all(jnp.broadcast_to(value[None], (count, *value.shape)), axis...  7.23 us
  transfers between devices with their start and end apart: 7, of which 7 were waited for; matrix products, arithmetic and copies ran while one was open for 2% of the time, Pallas kernels for 0%

commit v1 on v0

--- a/solution.py
+++ b/solution.py
@@ -111,17 +111,28 @@
     grad_bins[...] = jnp.zeros_like(grad_bins)
     side_sums[...] = jnp.zeros_like(side_sums)
 
-    w_in_half[...] = w_in_ref[...] * jnp.asarray(0.5, BF16)
+    w_in_half[0:width, :] = w_in_ref[...] * jnp.asarray(0.5, BF16)
+    rest = 0.5 * b_in_ref[...]
+    term_row = lax.broadcasted_iota(jnp.int32, (width, rest.shape[1]), 0)
+    terms = jnp.zeros(term_row.shape, F32)
+    for n in range(3):
+        term = rest.astype(BF16).astype(F32)
+        terms = jnp.where(term_row == n, term, terms)
+        rest = rest - term
+    w_in_half[width:, :] = terms.astype(BF16)
     w_out_half[...] = w_out_ref[...] * jnp.asarray(0.5, BF16)
     gain = gain_ref[...]
     bias = bias_ref[...]
-    b_in = 0.5 * b_in_ref[...]
     sub = lax.broadcasted_iota(jnp.int32, (GROUP, width), 0)
     lane = lax.broadcasted_iota(jnp.int32, (GROUP, width), 1)
     near = [sub >= ii + skew for ii in range(GROUP)]
     bin_lane = lax.broadcasted_iota(jnp.int32, (GROUP, w_bins_ref.shape[1]), 1).astype(F32)
     span = GROUP * half
     every = span + GROUP
+
+    ones_of = jnp.where(
+        lax.broadcasted_iota(jnp.int32, (2 * every, width), 1) < 3, 1.0, 0.0
+    ).astype(BF16)
 
     def step(s, carry):
         first = pl.multiple_of(s * GROUP, GROUP)
@@ -152,7 +163,7 @@
         inv_scale = lax.rsqrt(jnp.mean(center * center, axis=-1, keepdims=True) + 1e-05)
         normal_form = center * inv_scale
         normed = (normal_form * gain + bias).astype(BF16)
-        act = dot(normed, w_in_half[...]) + b_in
+        act = dot(jnp.concatenate([normed, ones_of], axis=1), w_in_half[...])
         up = jnp.tanh(act) + 1.0
         hidden = (act * up).astype(BF16)
         slope = up * (act * (2.0 - up) + 1.0)
@@ -267,7 +278,7 @@
         in_specs=[smem] + [vmem] * 9,
         out_specs=(vmem,) * 5,
         scratch_shapes=[
-            pltpu.VMEM((width, hidden), BF16),
+            pltpu.VMEM((2 * width, hidden), BF16),
             pltpu.VMEM((hidden, width), BF16),
             pltpu.VMEM((2, block, width), F32),
             pltpu.VMEM((2, block, width), F32),

time: 131 us -> 129 us (0.985)
  Pallas kernels: 32.3 us -> 30.5 us
    pallas_call x1, Pallas kernels: 32.3 us -> 30.5 us  [run_pairs(): pl.pallas_call(functools.partial(pair_kernel, count=count, rows=rows), ou...]
where the time goes in v1:
time: 129 us
  waiting for transfers between devices  35.7 us (28%)
  starting transfers between devices  35.5 us (28%)
  Pallas kernels  30.5 us (24%)
  blocking collectives  17.7 us (14%)
  local copies, waits for them, and re-layouts  5.72 us (4%)
  other arithmetic  2.87 us (2%)
    pallas_call x1, Pallas kernels, run_pairs(): pl.pallas_call(functools.partial(pair_kernel, count=count, rows=rows), ou...  30.5 us
    all_to_all x1, blocking collectives, on_device(): pieces = lax.all_to_all(pieces, 'row', 0, 0, tiled=True)  17.7 us
    all_to_all x2, starting transfers between devices, from_everyone(): lax.all_to_all(jnp.broadcast_to(value[None], (count, *value.shape)), axis...  10.9 us
    all_to_all x1, waiting for transfers between devices, on_device(): last = lax.all_to_all(last, 'col', 0, 0, tiled=True)  10.5 us
    all_to_all x1, starting transfers between devices, on_device(): shares = lax.all_to_all(col_out, 'col', 0, 0, tiled=True)  9.5 us
    all_to_all x1, starting transfers between devices, on_device(): last = lax.all_to_all(last, 'col', 0, 0, tiled=True)  7.76 us
    ppermute x1, waiting for transfers between devices, on_device(): far_right = lax.ppermute(far_right, both, routes)  7.35 us
    all_to_all x2, waiting for transfers between devices, from_everyone(): lax.all_to_all(jnp.broadcast_to(value[None], (count, *value.shape)), axis...  7.24 us
  transfers between devices with their start and end apart: 7, of which 7 were waited for; matrix products, arithmetic and copies ran while one was open for 2% of the time, Pallas kernels for 0%

profile of v1, /device:TPU:1, one launch (start us, length us, event | category | flops | bytes accessed | tf_op | source)
XLA Modules:
  0.0 128.7 jit_solution(12628859482485190977)
XLA Ops:
  0.6 0.7 pad_maximum_fusion.2
  1.4 0.6 broadcast_in_dim.15
  2.0 0.0 copy-start.5
  2.0 7.3 %all-to-all-start = ((bf16[16,16,128]{2,1,0:T(8,128)(2,1)}), bf16[16,16,128]{2,1,0:T(8,128)(2,1)S(1)}, u32[]{:S(2)}, u32[]{:S(2)}) async-start(bf16[16,16,128]{2,1,0:T(8,128)(2,1)} %broadcast_in_dim.15), calls=%async_computation | async-start | bytes 131072 | tf_op jit(solution)/shard_map/all_to_all | solution.py:18
  9.3 0.0 copy-start.2
  9.3 0.0 copy-done.5
  9.3 0.7 copy.21.w_bins_ref
  10.0 0.1 copy-done.2
  10.1 0.1 copy.20
  10.2 0.6 pad.8.labels_ref
  10.8 4.3 %all-to-all-done.mine_ref = bf16[16,16,128]{2,1,0:T(8,128)(2,1)S(1)} async-done(((bf16[16,16,128]{2,1,0:T(8,128)(2,1)}), bf16[16,16,128]{2,1,0:T(8,128)(2,1)S(1)}, u32[]{:S(2)}, u32[]{:S(2)}) %all-to-all-start) | async-done | bytes 65568 | tf_op jit(solution)/shard_map/all_to_all | solution.py:18
  15.1 0.0 copy-start
  15.1 3.2 %collective-permute-start = (bf16[16,16,128]{2,1,0:T(8,128)(2,1)S(1)}, bf16[16,16,128]{2,1,0:T(8,128)(2,1)S(1)}, u32[]{:S(2)}, u32[]{:S(2)}) collective-permute-start(bf16[16,16,128]{2,1,0:T(8,128)(2,1)S(1)} %all-to-all-done.mine_ref), channel_id=1, source_target_pairs={{9,0},{24,1},{41,2},{58,3},{65,4},{80,5},{97,6},{114,7},{137,8},{1... | collective-permute-start | bytes 196616 | tf_op jit(solution)/shard_map/ppermute | solution.py:324
  18.4 0.6 pad_add_fusion.place
  18.9 3.3 %collective-permute-done.theirs_ref = bf16[16,16,128]{2,1,0:T(8,128)(2,1)S(1)} collective-permute-done((bf16[16,16,128]{2,1,0:T(8,128)(2,1)S(1)}, bf16[16,16,128]{2,1,0:T(8,128)(2,1)S(1)}, u32[]{:S(2)}, u32[]{:S(2)}) %collective-permute-start) | collective-permute-done | bytes 65568 | tf_op jit(solution)/shard_map/ppermute | solution.py:324
  22.2 0.0 copy-start.1
  22.2 0.0 copy-done
  22.2 0.6 copy-done.1
  22.8 30.5 %pairs.1 = (f32[16,72,128]{2,1,0:T(8,128)}, f32[96,128]{1,0:T(8,128)}, f32[96,128]{1,0:T(8,128)}, f32[96,128]{1,0:T(8,128)}, f32[96,128]{1,0:T(8,128)}) custom-call(s32[2]{0:T(128)} %pad_add_fusion.place, bf16[16,16,128]{2,1,0:T(8,128)(2,1)} %copy-done, bf16[16,16,128]{2,1,0:T(8,128)(2,1)} %copy-done.1, f32[96,128]{1,0:T(8,128)} %pad.8.labels_ref, ...), custom_call_target="tpu_custom_call" | custom-call | tf_op jit(solution)/shard_map/pairs/pallas_call | solution.py:272
  53.3 0.0 copy-start.7
  53.3 0.0 copy-start.4
  53.3 9.5 %all-to-all-start.1 = ((f32[16,72,128]{2,1,0:T(8,128)}), f32[16,72,128]{2,1,0:T(8,128)S(1)}, u32[]{:S(2)}, u32[]{:S(2)}) async-start(f32[16,72,128]{2,1,0:T(8,128)} %get-tuple-element.10), calls=%async_computation.1 | async-start | bytes 1179648 | tf_op jit(solution)/shard_map/all_to_all | solution.py:330
  62.8 0.0 copy-done.7
  62.8 0.1 collective-permute-start.1
  62.9 7.4 %collective-permute-done.1 = f32[96,128]{1,0:T(8,128)S(1)} collective-permute-done((f32[96,128]{1,0:T(8,128)S(1)}, f32[96,128]{1,0:T(8,128)S(1)}, u32[]{:S(2)}, u32[]{:S(2)}) %collective-permute-start.1) | collective-permute-done | bytes 49184 | tf_op jit(solution)/shard_map/ppermute | solution.py:332
  70.3 0.0 copy-done.4
  70.3 4.6 %all-to-all-done.1 = f32[16,72,128]{2,1,0:T(8,128)S(1)} async-done(((f32[16,72,128]{2,1,0:T(8,128)}), f32[16,72,128]{2,1,0:T(8,128)S(1)}, u32[]{:S(2)}, u32[]{:S(2)}) %all-to-all-start.1) | async-done | bytes 589856 | tf_op jit(solution)/shard_map/all_to_all | solution.py:330
  75.0 17.7 %all_to_all.25 = f32[16,11,128]{2,1,0:T(8,128)S(1)} all-to-all(f32[16,11,128]{2,1,0:T(8,128)S(1)} %pad_maximum_fusion.1), channel_id=1, replica_groups=mesh['row'=16,'col'=16] {'row'}, dimensions={0} | all-to-all | bytes 180224 | tf_op jit(solution)/shard_map/all_to_all | solution.py:345
  92.8 0.7 broadcast_in_dim.35
  93.5 0.0 copy-start.6
  93.5 0.0 copy-start.3
  93.5 3.6 %all-to-all-start.3 = ((f32[16,11,128]{2,1,0:T(8,128)}), f32[16,11,128]{2,1,0:T(8,128)S(1)}, u32[]{:S(2)}, u32[]{:S(2)}) async-start(f32[16,11,128]{2,1,0:T(8,128)} %broadcast_in_dim.35), calls=%async_computation.3 | async-start | bytes 262144 | tf_op jit(solution)/shard_map/all_to_all | solution.py:18
  97.1 0.0 copy-done.6
  97.1 3.9 %collective-permute-start.2 = (f32[96,128]{1,0:T(8,128)S(1)}, f32[96,128]{1,0:T(8,128)S(1)}, u32[]{:S(2)}, u32[]{:S(2)}) collective-permute-start(f32[96,128]{1,0:T(8,128)S(1)} %copy-done.6), channel_id=1, source_target_pairs={{0,9},{1,24},{2,41},{3,58},{4,65},{5,80},{6,97},{7,114},{8,137},{9... | collective-permute-start | bytes 147464 | tf_op jit(solution)/shard_map/ppermute | solution.py:347
  101.0 2.7 %collective-permute-done.2 = f32[96,128]{1,0:T(8,128)S(1)} collective-permute-done((f32[96,128]{1,0:T(8,128)S(1)}, f32[96,128]{1,0:T(8,128)S(1)}, u32[]{:S(2)}, u32[]{:S(2)}) %collective-permute-start.2) | collective-permute-done | bytes 49184 | tf_op jit(solution)/shard_map/ppermute | solution.py:347
  103.8 0.0 copy-done.3
  103.8 2.9 %all-to-all-done.3 = f32[16,11,128]{2,1,0:T(8,128)S(1)} async-done(((f32[16,11,128]{2,1,0:T(8,128)}), f32[16,11,128]{2,1,0:T(8,128)S(1)}, u32[]{:S(2)}, u32[]{:S(2)}) %all-to-all-start.3) | async-done | bytes 90144 | tf_op jit(solution)/shard_map/all_to_all | solution.py:18
  106.8 0.9 pad_maximum_fusion
  107.7 7.8 %all-to-all-start.4 = ((f32[16,78,128]{2,1,0:T(8,128)}), f32[16,78,128]{2,1,0:T(8,128)S(1)}, u32[]{:S(2)}, u32[]{:S(2)}) async-start(f32[16,78,128]{2,1,0:T(8,128)} %pad_maximum_fusion), calls=%async_computation.4 | async-start | bytes 1310720 | tf_op jit(solution)/shard_map/all_to_all | solution.py:362
  115.5 0.6 reshape.43
  116.1 10.5 %all-to-all-done.4 = f32[16,78,128]{2,1,0:T(8,128)S(1)} async-done(((f32[16,78,128]{2,1,0:T(8,128)}), f32[16,78,128]{2,1,0:T(8,128)S(1)}, u32[]{:S(2)}, u32[]{:S(2)}) %all-to-all-start.4) | async-done | bytes 639008 | tf_op jit(solution)/shard_map/all_to_all | solution.py:362
  126.6 0.7 copy.22
  127.3 0.6 slice_reduce_fusion
  127.9 0.9 fusion
  (17 shorter events, 0.2 us)
Async XLA Ops:
  2.0 7.3 %copy-start.5 = (bf16[128,64]{0,1:T(8,128)(2,1)S(1)}, bf16[128,64]{0,1:T(8,128)(2,1)}, u32[]{:S(2)}) copy-start(bf16[128,64]{0,1:T(8,128)(2,1)} %param.16) | copy-start | bytes 49156
  2.0 13.1 %all-to-all-start = ((bf16[16,16,128]{2,1,0:T(8,128)(2,1)}), bf16[16,16,128]{2,1,0:T(8,128)(2,1)S(1)}, u32[]{:S(2)}, u32[]{:S(2)}) async-start(bf16[16,16,128]{2,1,0:T(8,128)(2,1)} %broadcast_in_dim.15), calls=%async_computation | async-start | bytes 131072 | tf_op jit(solution)/shard_map/all_to_all | solution.py:18
  9.3 0.8 copy-start.2
  15.1 7.1 %copy-start = (bf16[16,16,128]{2,1,0:T(8,128)(2,1)}, bf16[16,16,128]{2,1,0:T(8,128)(2,1)S(1)}, u32[]{:S(2)}) copy-start(bf16[16,16,128]{2,1,0:T(8,128)(2,1)S(1)} %all-to-all-done.mine_ref) | copy-start | bytes 196612
  15.1 7.1 %collective-permute-start = (bf16[16,16,128]{2,1,0:T(8,128)(2,1)S(1)}, bf16[16,16,128]{2,1,0:T(8,128)(2,1)S(1)}, u32[]{:S(2)}, u32[]{:S(2)}) collective-permute-start(bf16[16,16,128]{2,1,0:T(8,128)(2,1)S(1)} %all-to-all-done.mine_ref), channel_id=1, source_target_pairs={{9,0},{24,1},{41,2},{58,3},{65,4},{80,5},{97,6},{114,7},{137,8},{1... | collective-permute-start | bytes 196616 | tf_op jit(solution)/shard_map/ppermute | solution.py:324
  22.2 0.6 copy-start.1
  53.3 9.5 %copy-start.7 = (f32[96,128]{1,0:T(8,128)S(1)}, f32[96,128]{1,0:T(8,128)}, u32[]{:S(2)}) copy-start(f32[96,128]{1,0:T(8,128)} %get-tuple-element.12) | copy-start | bytes 147460
  53.3 17.0 %copy-start.4 = (f32[96,128]{1,0:T(8,128)S(1)}, f32[96,128]{1,0:T(8,128)}, u32[]{:S(2)}) copy-start(f32[96,128]{1,0:T(8,128)} %get-tuple-element.11) | copy-start | bytes 147460
  53.3 21.6 %all-to-all-start.1 = ((f32[16,72,128]{2,1,0:T(8,128)}), f32[16,72,128]{2,1,0:T(8,128)S(1)}, u32[]{:S(2)}, u32[]{:S(2)}) async-start(f32[16,72,128]{2,1,0:T(8,128)} %get-tuple-element.10), calls=%async_computation.1 | async-start | bytes 1179648 | tf_op jit(solution)/shard_map/all_to_all | solution.py:330
  62.8 7.5 %collective-permute-start.1 = (f32[96,128]{1,0:T(8,128)S(1)}, f32[96,128]{1,0:T(8,128)S(1)}, u32[]{:S(2)}, u32[]{:S(2)}) collective-permute-start(f32[96,128]{1,0:T(8,128)S(1)} %copy-done.7), channel_id=1, source_target_pairs={{9,0},{24,1},{41,2},{58,3},{65,4},{80,5},{97,6},{114,7},{137,8},{1... | collective-permute-start | bytes 147464 | tf_op jit(solution)/shard_map/ppermute | solution.py:332
  93.5 3.7 %copy-start.6 = (f32[96,128]{1,0:T(8,128)S(1)}, f32[96,128]{1,0:T(8,128)}, u32[]{:S(2)}) copy-start(f32[96,128]{1,0:T(8,128)} %get-tuple-element.14) | copy-start | bytes 147460
  93.5 10.3 %copy-start.3 = (f32[96,128]{1,0:T(8,128)S(1)}, f32[96,128]{1,0:T(8,128)}, u32[]{:S(2)}) copy-start(f32[96,128]{1,0:T(8,128)} %get-tuple-element.13) | copy-start | bytes 147460
  93.5 13.3 %all-to-all-start.3 = ((f32[16,11,128]{2,1,0:T(8,128)}), f32[16,11,128]{2,1,0:T(8,128)S(1)}, u32[]{:S(2)}, u32[]{:S(2)}) async-start(f32[16,11,128]{2,1,0:T(8,128)} %broadcast_in_dim.35), calls=%async_computation.3 | async-start | bytes 262144 | tf_op jit(solution)/shard_map/all_to_all | solution.py:18
  97.1 6.6 %collective-permute-start.2 = (f32[96,128]{1,0:T(8,128)S(1)}, f32[96,128]{1,0:T(8,128)S(1)}, u32[]{:S(2)}, u32[]{:S(2)}) collective-permute-start(f32[96,128]{1,0:T(8,128)S(1)} %copy-done.6), channel_id=1, source_target_pairs={{0,9},{1,24},{2,41},{3,58},{4,65},{5,80},{6,97},{7,114},{8,137},{9... | collective-permute-start | bytes 147464 | tf_op jit(solution)/shard_map/ppermute | solution.py:347
  107.7 18.9 %all-to-all-start.4 = ((f32[16,78,128]{2,1,0:T(8,128)}), f32[16,78,128]{2,1,0:T(8,128)S(1)}, u32[]{:S(2)}, u32[]{:S(2)}) async-start(f32[16,78,128]{2,1,0:T(8,128)} %pad_maximum_fusion), calls=%async_computation.4 | async-start | bytes 1310720 | tf_op jit(solution)/shard_map/all_to_all | solution.py:362
